TPU v7x, 256 devices: a whole 4x4x8 slice. The times are simulated.
256 devices in a mesh: dp: 8 (over x, core), table: 32 (over y, z).
Axes of the slice: x: 4, y: 4, z: 8, core: 2. Of those that a mesh axis runs over, the one named last changes fastest.
Arguments:
- out_grad: bfloat16 [262144, 1024], P(('dp', 'table')), may hold values from -0.125 to 0.125
- pair_cells: int32 [262144, 8, 32], P(('dp', 'table')), may hold values from 0 to 4095
- weight_codes: int32 [262144, 8, 32], P(('dp', 'table')), may hold values from -127 to 127
- head_scale: float32 [8], replicated, may hold values from 0.5 to 2
- touch_slots: int32 [32, 32, 1], replicated, may hold values from 0 to 7
Outputs:
- grad_rows: bfloat16 [32768, 1024], P('table', 'dp')
All inputs are finite; a program needn't handle non-finite values.
Results may differ from a plain program's by a relative error of at most 0.0098.
Values may be sent and summed in bfloat16 or wider, within the bound.
A program may use at most 128 MiB of HBM per device.

v0:
```python
import jax
import jax.numpy as jnp
from jax import lax
from jax.sharding import PartitionSpec as P

ROWS = 128
TOUCH = 32
OWN = 8


def coef_table(cell_block, weight_block):
    block = cell_block.shape[0]
    pairs = cell_block.shape[1]
    inner = min(block, 128)
    tile_iota = jnp.arange(TOUCH, dtype=jnp.int32)
    row_iota = jnp.arange(ROWS, dtype=jnp.int32)

    def build(inputs):
        cell_part, weight_part = inputs
        tile_hot = (cell_part[:, :, None] // ROWS == tile_iota[None, None, :]).astype(
            jnp.float32
        ) * weight_part[:, :, None]
        row_hot = (cell_part[:, :, None] % ROWS == row_iota[None, None, :]).astype(jnp.float32)
        coef = jnp.einsum("tpj,tpr->tjr", tile_hot, row_hot, precision=lax.Precision.HIGHEST)
        return coef.reshape(inner, TOUCH * ROWS).astype(jnp.bfloat16)

    parts = lax.map(
        build,
        (
            cell_block.reshape(block // inner, inner, pairs),
            weight_block.reshape(block // inner, inner, pairs),
        ),
    )
    return parts.reshape(block, TOUCH * ROWS)


def tile_partial(cells, weights, grads):
    tokens = cells.shape[0]
    width = grads.shape[1]
    span = TOUCH * ROWS
    block = min(tokens, 512)
    blocks = tokens // block
    cell_blocks = cells.reshape(blocks, block, -1)
    weight_blocks = weights.reshape(blocks, block, -1)
    grad_blocks = grads.reshape(blocks, block, width)

    def accumulate(partial_value, inputs):
        cell_block, weight_block, grad_block = inputs
        coef = coef_table(cell_block, weight_block)
        return (
            partial_value
            + jnp.einsum("ts,tw->sw", coef, grad_block, preferred_element_type=jnp.float32),
            None,
        )

    partial_value, _ = lax.scan(
        accumulate, jnp.zeros((span, width), jnp.float32), (cell_blocks, weight_blocks, grad_blocks)
    )
    return partial_value


def body(out_grad, pair_cells, weight_codes, head_scale, touch_slots):
    tokens = out_grad.shape[0]
    groups = touch_slots.shape[0]
    capacity = touch_slots.shape[2]
    touched = groups * capacity
    group = lax.axis_index("table")
    pair_count = pair_cells.shape[1] * pair_cells.shape[2]
    mine = lax.dynamic_index_in_dim(touch_slots, group, 1, keepdims=False).reshape(touched)
    select = (mine[None, :] == jnp.arange(OWN, dtype=jnp.int32)[:, None]).astype(jnp.float32)
    weight = (weight_codes.astype(jnp.float32) * head_scale[None, :, None] / 128.0).reshape(
        tokens, pair_count
    )
    partial_value = tile_partial(pair_cells.reshape(tokens, pair_count), weight, out_grad)
    narrow = lax.psum_scatter(
        partial_value.astype(jnp.bfloat16), "dp", scatter_dimension=1, tiled=True
    ).astype(jnp.float32)
    sent = narrow.reshape(groups, capacity * ROWS, narrow.shape[1])
    received = lax.all_to_all(
        sent.astype(jnp.bfloat16), "table", split_axis=0, concat_axis=0, tiled=True
    ).astype(sent.dtype)
    owned = jnp.einsum("ks,srw->krw", select, received, precision=lax.Precision.HIGHEST)
    result = owned.reshape(OWN * ROWS, received.shape[2])
    return result.astype(jnp.bfloat16)


def solution(mesh):
    return jax.shard_map(
        body,
        mesh=mesh,
        in_specs=(
            P(("dp", "table"), None),
            P(("dp", "table"), None, None),
            P(("dp", "table"), None, None),
            P(),
            P(),
        ),
        out_specs=P("table", "dp"),
        check_vma=False,
    )
```

profile of v0, /device:TPU:32, one launch (start us, length us, event | category | flops | bytes accessed | tf_op | source)
XLA Modules:
  0.0 270.3 jit_solution(13635979526777270513)
XLA Ops:
  6.5 1.4 multiply_multiply_fusion
  8.0 0.9 reshape_reshape.7
  8.9 3.1 %reshape_reshape.6 = s32[2,512,256]{1,0,2:T(2,128)} reshape(s32[1024,8,32]{0,2,1:T(8,128)} %param.10) | data formatting | bytes 2097152 | tf_op jit(solution)/shard_map/reshape;reshape | solution.py:43
  12.0 131.5 %while.35 = (s32[]{:T(128)}, f32[4096,1024]{1,0:T(8,128)}, s32[2,512,256]{1,0,2:T(2,128)}, f32[2,512,256]{1,0,2:T(2,128)S(1)}, bf16[2,512,1024]{2,1,0:T(8,128)(2,1)}, /*index=5*/s32[]{:T(128)}, s32[]{:T(128)}, s32[]{:T(128)}) while((s32[]{:T(128)}, f32[4096,1024]{1,0:T(8,128)}, s32[2,512,256]{1,0,2:T(2,128)}, ...), condition=%wide.region_3.4_spmd.clone, body=%wide.region_0.3_spmd.clone.sunk | while | flops 5921603584 | bytes 57869592 | solution.py:56
  12.0 2.1 constant_dynamic-slice_fusion.4
  14.0 0.5 copy.24
  14.5 0.5 constant_dynamic-slice_fusion.5
  15.0 0.5 copy.25
  15.5 46.8 %while.36 = (s32[]{:T(128)}, bf16[4,128,4096]{2,1,0:T(8,128)(2,1)}, s32[4,128,256]{2,1,0:T(8,128)S(1)}, f32[4,128,256]{2,1,0:T(8,128)S(1)}, s32[]{:T(128)}) while((s32[]{:T(128)}, bf16[4,128,4096]{2,1,0:T(8,128)(2,1)}, s32[4,128,256]{2,1,0:T(8,128)S(1)}, f32[4,128,256]{2,1,0:T(8,128)S(1)}, s32[]{:T(128)}) %tuple.76), condition=%wide.region_2.2_spmd.clone, body=%wide.region_1.1_spmd.clone.sunk | while | flops 1618247680 | bytes 6488649 | solution.py:27
  15.7 9.9 %fusion.32 = bf16[128,32,128]{2,1,0:T(8,128)(2,1)S(1)} fusion(s32[128,256]{1,0:T(8,128)S(1)} %add_select_fusion.5, f32[128,256]{1,0:T(8,128)S(1)} %dynamic-slice_bitcast_fusion.2, s32[128,256]{1,0:T(8,128)S(1)} %get-tuple-element.296), kind=kOutput, calls=%fused_computation.10.clone.1 | convolution fusion | flops 1617428480 | bytes 1441792 | tf_op jit(solution)/shard_map/while/body/eval_jaxpr/while/body/eval_jaxpr/tpj,tpr->tjr/dot_general | solution.py:24
  25.7 0.5 convert_element_type.50
  26.2 1.1 constant_dynamic-update-slice_fusion.2
  27.4 9.9 %fusion.32 = bf16[128,32,128]{2,1,0:T(8,128)(2,1)S(1)} fusion(s32[128,256]{1,0:T(8,128)S(1)} %add_select_fusion.5, f32[128,256]{1,0:T(8,128)S(1)} %dynamic-slice_bitcast_fusion.2, s32[128,256]{1,0:T(8,128)S(1)} %get-tuple-element.296), kind=kOutput, calls=%fused_computation.10.clone.1 | convolution fusion | flops 1617428480 | bytes 1441792 | tf_op jit(solution)/shard_map/while/body/eval_jaxpr/while/body/eval_jaxpr/tpj,tpr->tjr/dot_general | solution.py:24
  37.4 0.5 convert_element_type.50
  37.9 1.1 constant_dynamic-update-slice_fusion.2
  39.1 9.9 %fusion.32 = bf16[128,32,128]{2,1,0:T(8,128)(2,1)S(1)} fusion(s32[128,256]{1,0:T(8,128)S(1)} %add_select_fusion.5, f32[128,256]{1,0:T(8,128)S(1)} %dynamic-slice_bitcast_fusion.2, s32[128,256]{1,0:T(8,128)S(1)} %get-tuple-element.296), kind=kOutput, calls=%fused_computation.10.clone.1 | convolution fusion | flops 1617428480 | bytes 1441792 | tf_op jit(solution)/shard_map/while/body/eval_jaxpr/while/body/eval_jaxpr/tpj,tpr->tjr/dot_general | solution.py:24
  49.1 0.5 convert_element_type.50
  49.6 1.1 constant_dynamic-update-slice_fusion.2
  50.8 9.9 %fusion.32 = bf16[128,32,128]{2,1,0:T(8,128)(2,1)S(1)} fusion(s32[128,256]{1,0:T(8,128)S(1)} %add_select_fusion.5, f32[128,256]{1,0:T(8,128)S(1)} %dynamic-slice_bitcast_fusion.2, s32[128,256]{1,0:T(8,128)S(1)} %get-tuple-element.296), kind=kOutput, calls=%fused_computation.10.clone.1 | convolution fusion | flops 1617428480 | bytes 1441792 | tf_op jit(solution)/shard_map/while/body/eval_jaxpr/while/body/eval_jaxpr/tpj,tpr->tjr/dot_general | solution.py:24
  60.8 0.5 convert_element_type.50
  61.3 1.1 constant_dynamic-update-slice_fusion.2
  62.3 13.0 %select_add_fusion.2 = f32[4096,1024]{1,0:T(8,128)} fusion(f32[4096,1024]{1,0:T(8,128)} %get-tuple-element.321, pred[]{:T(512)S(6)} %compare.18, bf16[512,4096]{1,0:T(8,128)(2,1)} %bitcast.60, bf16[2,512,1024]{2,1,0:T(8,128)(2,1)} %get-tuple-element.332, s32[]{:T(128)} %get-tuple-element.320), kind=kOutput, calls=%fused_computation.24.clone.1 | convolution fusion | flops 4303355904 | bytes 38797824 | tf_op jit(solution)/shard_map/while/body/eval_jaxpr/ts,tw->sw/dot_general | solution.py:52
  75.3 2.1 constant_dynamic-slice_fusion.4
  77.4 0.5 copy.24
  78.3 0.5 copy.25
  78.9 46.8 %while.36 = (s32[]{:T(128)}, bf16[4,128,4096]{2,1,0:T(8,128)(2,1)}, s32[4,128,256]{2,1,0:T(8,128)S(1)}, f32[4,128,256]{2,1,0:T(8,128)S(1)}, s32[]{:T(128)}) while((s32[]{:T(128)}, bf16[4,128,4096]{2,1,0:T(8,128)(2,1)}, s32[4,128,256]{2,1,0:T(8,128)S(1)}, f32[4,128,256]{2,1,0:T(8,128)S(1)}, s32[]{:T(128)}) %tuple.76), condition=%wide.region_2.2_spmd.clone, body=%wide.region_1.1_spmd.clone.sunk | while | flops 1618247680 | bytes 6488649 | solution.py:27
  79.1 9.9 %fusion.32 = bf16[128,32,128]{2,1,0:T(8,128)(2,1)S(1)} fusion(s32[128,256]{1,0:T(8,128)S(1)} %add_select_fusion.5, f32[128,256]{1,0:T(8,128)S(1)} %dynamic-slice_bitcast_fusion.2, s32[128,256]{1,0:T(8,128)S(1)} %get-tuple-element.296), kind=kOutput, calls=%fused_computation.10.clone.1 | convolution fusion | flops 1617428480 | bytes 1441792 | tf_op jit(solution)/shard_map/while/body/eval_jaxpr/while/body/eval_jaxpr/tpj,tpr->tjr/dot_general | solution.py:24
  89.0 0.5 convert_element_type.50
  89.5 1.1 constant_dynamic-update-slice_fusion.2
  90.7 9.9 %fusion.32 = bf16[128,32,128]{2,1,0:T(8,128)(2,1)S(1)} fusion(s32[128,256]{1,0:T(8,128)S(1)} %add_select_fusion.5, f32[128,256]{1,0:T(8,128)S(1)} %dynamic-slice_bitcast_fusion.2, s32[128,256]{1,0:T(8,128)S(1)} %get-tuple-element.296), kind=kOutput, calls=%fused_computation.10.clone.1 | convolution fusion | flops 1617428480 | bytes 1441792 | tf_op jit(solution)/shard_map/while/body/eval_jaxpr/while/body/eval_jaxpr/tpj,tpr->tjr/dot_general | solution.py:24
  100.7 0.5 convert_element_type.50
  101.2 1.1 constant_dynamic-update-slice_fusion.2
  102.5 9.9 %fusion.32 = bf16[128,32,128]{2,1,0:T(8,128)(2,1)S(1)} fusion(s32[128,256]{1,0:T(8,128)S(1)} %add_select_fusion.5, f32[128,256]{1,0:T(8,128)S(1)} %dynamic-slice_bitcast_fusion.2, s32[128,256]{1,0:T(8,128)S(1)} %get-tuple-element.296), kind=kOutput, calls=%fused_computation.10.clone.1 | convolution fusion | flops 1617428480 | bytes 1441792 | tf_op jit(solution)/shard_map/while/body/eval_jaxpr/while/body/eval_jaxpr/tpj,tpr->tjr/dot_general | solution.py:24
  112.4 0.5 convert_element_type.50
  112.9 1.1 constant_dynamic-update-slice_fusion.2
  114.2 9.9 %fusion.32 = bf16[128,32,128]{2,1,0:T(8,128)(2,1)S(1)} fusion(s32[128,256]{1,0:T(8,128)S(1)} %add_select_fusion.5, f32[128,256]{1,0:T(8,128)S(1)} %dynamic-slice_bitcast_fusion.2, s32[128,256]{1,0:T(8,128)S(1)} %get-tuple-element.296), kind=kOutput, calls=%fused_computation.10.clone.1 | convolution fusion | flops 1617428480 | bytes 1441792 | tf_op jit(solution)/shard_map/while/body/eval_jaxpr/while/body/eval_jaxpr/tpj,tpr->tjr/dot_general | solution.py:24
  124.1 0.5 convert_element_type.50
  124.6 1.1 constant_dynamic-update-slice_fusion.2
  125.7 17.8 %select_add_fusion.2 = f32[4096,1024]{1,0:T(8,128)} fusion(f32[4096,1024]{1,0:T(8,128)} %get-tuple-element.321, pred[]{:T(512)S(6)} %compare.18, bf16[512,4096]{1,0:T(8,128)(2,1)} %bitcast.60, bf16[2,512,1024]{2,1,0:T(8,128)(2,1)} %get-tuple-element.332, s32[]{:T(128)} %get-tuple-element.320), kind=kOutput, calls=%fused_computation.24.clone.1 | convolution fusion | flops 4303355904 | bytes 38797824 | tf_op jit(solution)/shard_map/while/body/eval_jaxpr/ts,tw->sw/dot_general | solution.py:52
  143.5 9.1 %convert_element_type.38 = bf16[4096,1024]{1,0:T(8,128)(2,1)} convert(f32[4096,1024]{1,0:T(8,128)} %get-tuple-element.165) | non-fusion elementwise | flops 4194304 | bytes 25165824 | tf_op jit(solution)/shard_map/convert_element_type | solution.py:76
  152.6 11.3 %copy.16 = bf16[4096,1024]{0,1:T(8,128)(2,1)} copy(bf16[4096,1024]{1,0:T(8,128)(2,1)} %convert_element_type.38) | data formatting | bytes 16777216
  163.9 57.7 %reduce-scatter.4.cloned.1.call-done = bf16[128,4096]{1,0:T(8,128)(2,1)} async-done(((bf16[1024,4096]{1,0:T(8,128)(2,1)}), bf16[128,4096]{1,0:T(8,128)(2,1)}) %reduce-scatter.4.cloned.1.call-update) | async-done | bytes 1048592
  221.7 2.3 copy.17
  223.9 10.1 %all-to-all-start = ((bf16[32,128,128]{2,1,0:T(8,128)(2,1)}), bf16[32,128,128]{2,1,0:T(8,128)(2,1)S(1)}, u32[]{:S(2)}, u32[]{:S(2)}) async-start(bf16[32,128,128]{2,1,0:T(8,128)(2,1)} %bitcast.2), calls=%async_computation | async-start | bytes 2097152 | tf_op jit(solution)/shard_map/all_to_all | solution.py:79
  234.0 0.7 dynamic-slice_reduce_fusion
  234.8 27.3 %all-to-all-done = bf16[32,128,128]{2,1,0:T(8,128)(2,1)S(1)} async-done(((bf16[32,128,128]{2,1,0:T(8,128)(2,1)}), bf16[32,128,128]{2,1,0:T(8,128)(2,1)S(1)}, u32[]{:S(2)}, u32[]{:S(2)}) %all-to-all-start) | async-done | bytes 1048608 | tf_op jit(solution)/shard_map/all_to_all | solution.py:79
  262.0 0.7 convolution_convert_fusion
  262.7 0.8 copy.15
  (40 shorter events, 1.8 us)
Async XLA Ops:
  6.5 227.5 %copy-start = (s32[32,32,1]{1,2,0:T(1,128)S(1)}, s32[32,32,1]{1,2,0:T(1,128)}, u32[]{:S(2)}) copy-start(s32[32,32,1]{1,2,0:T(1,128)} %param.13) | copy-start | bytes 12292
  6.5 215.1 %reduce-scatter.4.cloned.1.call-start = ((), (), s32[]{:S(2)}) async-start(), calls=%async_computation.2 | async-start | bytes 9437184
  12.0 3.5 %copy-start.1 = (f32[2,512,256]{1,0,2:T(2,128)}, f32[2,512,256]{1,0,2:T(2,128)S(1)}, u32[]{:S(2)}) copy-start(f32[2,512,256]{1,0,2:T(2,128)S(1)} %get-tuple-element.331) | copy-start | bytes 3145732 | tf_op jit(solution)/shard_map/while
  62.3 13.0 %copy-start.2 = (f32[2,512,256]{1,0,2:T(2,128)S(1)}, f32[2,512,256]{1,0,2:T(2,128)}, u32[]{:S(2)}) copy-start(f32[2,512,256]{1,0,2:T(2,128)} %copy-done.1) | copy-start | bytes 3145732 | tf_op jit(solution)/shard_map/while
  75.3 3.5 %copy-start.1 = (f32[2,512,256]{1,0,2:T(2,128)}, f32[2,512,256]{1,0,2:T(2,128)S(1)}, u32[]{:S(2)}) copy-start(f32[2,512,256]{1,0,2:T(2,128)S(1)} %get-tuple-element.331) | copy-start | bytes 3145732 | tf_op jit(solution)/shard_map/while
  125.7 17.8 %copy-start.2 = (f32[2,512,256]{1,0,2:T(2,128)S(1)}, f32[2,512,256]{1,0,2:T(2,128)}, u32[]{:S(2)}) copy-start(f32[2,512,256]{1,0,2:T(2,128)} %copy-done.1) | copy-start | bytes 3145732 | tf_op jit(solution)/shard_map/while
  223.9 38.1 %all-to-all-start = ((bf16[32,128,128]{2,1,0:T(8,128)(2,1)}), bf16[32,128,128]{2,1,0:T(8,128)(2,1)S(1)}, u32[]{:S(2)}, u32[]{:S(2)}) async-start(bf16[32,128,128]{2,1,0:T(8,128)(2,1)} %bitcast.2), calls=%async_computation | async-start | bytes 2097152 | tf_op jit(solution)/shard_map/all_to_all | solution.py:79
Sparse Core Ops, SparseCore 0:
  164.1 57.5 reduce-scatter.3
where the time goes:
time: 271 us; the launch traced here: 270 us
  matrix products  111 us (41%)
  waiting for transfers between devices  85 us (31%)
  local copies, waits for them, and re-layouts  38.7 us (14%)
  between operations  13.4 us (5%)
  other arithmetic  11.7 us (4%)
  starting transfers between devices  10.1 us (4%)
    dot_general x8, matrix products, build(): jnp.einsum('tpj,tpr->tjr', tile_hot, row_hot, precision=lax.Precision.HIG...  79.5 us
    unnamed x2, waiting for transfers between devices  57.7 us
    dot_general x2, matrix products, accumulate(): jnp.einsum('ts,tw->sw', coef, grad_block, preferred_element_type=jnp.floa...  30.8 us
    all_to_all x1, waiting for transfers between devices, body(): lax.all_to_all(sent.astype(jnp.bfloat16), 'table', split_axis=0, concat_a...  27.3 us
    unnamed x4, local copies, waits for them, and re-layouts  13.6 us
    all_to_all x1, starting transfers between devices, body(): lax.all_to_all(sent.astype(jnp.bfloat16), 'table', split_axis=0, concat_a...  10.1 us
    convert_element_type x1, other arithmetic, body(): partial_value.astype(jnp.bfloat16)  9.1 us
    dynamic_update_slice x8, local copies, waits for them, and re-layouts, coef_table(): lax.map(build, (cell_block.reshape(block // inner, inner, pairs), weight_...  8.53 us
  transfers between devices with their start and end apart: 2, of which 2 were waited for; matrix products, arithmetic and copies ran while one was open for 0% of the time, Pallas kernels for 0%

commit v1 on v0

v1 whole, which is shorter than its diff:
```python
import functools

import jax
import jax.numpy as jnp
from jax import lax
from jax.experimental import pallas as pl
from jax.experimental.pallas import tpu as pltpu
from jax.sharding import PartitionSpec as P

ROWS = 128
TOUCH = 32
OWN = 8
NX = 4
NY = 4
NZ = 8
MESH = pl.DeviceIdType.MESH
BF = jnp.bfloat16
F32 = jnp.float32


def coef_kernel(block, unroll, stride, scale_ref, cells_ref, codes_ref, grad_ref, coef_ref, gt_ref,
                row_ref, tile_ref, weight_ref, table_ref):
    pairs = cells_ref.shape[0]
    heads = scale_ref.shape[0]
    per = pairs // heads
    cells = cells_ref[...]
    row_ref[...] = (cells % ROWS).astype(F32).T.astype(BF)
    tile_ref[...] = (cells // ROWS).astype(F32).T.astype(BF)
    weight = jnp.concatenate(
        [
            codes_ref[h * per : (h + 1) * per, :].astype(F32) * (scale_ref[h] / 128.0)
            for h in range(heads)
        ],
        axis=0,
    )
    weight_ref[...] = weight.T.astype(BF)
    for b in range(grad_ref.shape[1] // ROWS):
        gt_ref[b * ROWS : (b + 1) * ROWS, :] = grad_ref[:, b * ROWS : (b + 1) * ROWS].T
    row_iota = lax.broadcasted_iota(jnp.int32, (ROWS, pairs), 0).astype(F32).astype(BF)
    tile_iota = lax.broadcasted_iota(jnp.int32, (TOUCH, pairs), 0).astype(F32).astype(BF)
    one = jnp.ones((), BF)
    zero = jnp.zeros((), BF)

    def step(g, carry):
        base = pl.multiple_of(g * unroll, unroll)
        row = row_ref[pl.ds(base, unroll), :]
        tile = tile_ref[pl.ds(base, unroll), :]
        weights = weight_ref[pl.ds(base, unroll), :]
        for u in range(unroll):
            row_hot = jnp.where(
                jnp.broadcast_to(row[u : u + 1, :], (ROWS, pairs)) == row_iota, one, zero
            ).astype(jnp.float8_e4m3fn)
            tile_hot = jnp.where(
                jnp.broadcast_to(tile[u : u + 1, :], (TOUCH, pairs)) == tile_iota,
                jnp.broadcast_to(weights[u : u + 1, :], (TOUCH, pairs)),
                zero,
            )
            table_ref[pl.ds(base + u, TOUCH, stride=stride), :] = lax.dot_general(
                tile_hot, row_hot, (((1,), (1,)), ((), ())), preferred_element_type=F32
            )
        return carry

    lax.fori_loop(0, block // unroll, step, 0)

    def flush(j, carry):
        coef_ref[j] = table_ref[pl.ds(pl.multiple_of(j * stride, 8), block), :].astype(BF)
        return carry

    lax.fori_loop(0, TOUCH, flush, 0, unroll=8)


def coef_tables(cells, codes, head_scale, out_grad, block=128, unroll=64):
    pairs, tokens = cells.shape
    width = out_grad.shape[1]
    stride = block + 8
    return pl.pallas_call(
        functools.partial(coef_kernel, block, unroll, stride),
        grid=(tokens // block,),
        in_specs=[
            pl.BlockSpec(memory_space=pltpu.SMEM),
            pl.BlockSpec((pairs, block), lambda i: (0, i)),
            pl.BlockSpec((pairs, block), lambda i: (0, i)),
            pl.BlockSpec((block, width), lambda i: (i, 0)),
        ],
        out_specs=[
            pl.BlockSpec((TOUCH, block, ROWS), lambda i: (0, i, 0)),
            pl.BlockSpec((width, block), lambda i: (0, i)),
        ],
        out_shape=[
            jax.ShapeDtypeStruct((TOUCH, tokens, ROWS), BF),
            jax.ShapeDtypeStruct((width, tokens), BF),
        ],
        scratch_shapes=[pltpu.VMEM((block, pairs), BF)] * 3
        + [pltpu.VMEM((TOUCH * stride, ROWS), F32)],
        compiler_params=pltpu.CompilerParams(vmem_limit_bytes=48 << 20),
        name="coef_tables",
    )(head_scale, cells, codes, out_grad)


def exchange_kernel(slots_ref, coef_ref, gt_ref, out_ref,
                    grads, coefs, own, pair_out, pair_in,
                    opp_out, opp_in, near_out, near_in, keep, fin0, tiles, got, acc,
                    grad_sem, coef_sem, pair_send, pair_recv,
                    opp_send, opp_recv, near_send, near_recv, tile_send, tile_recv):
    dp = lax.axis_index("dp")
    table = lax.axis_index("table")
    x, c = lax.div(dp, 2), lax.rem(dp, 2)
    y, z = lax.div(table, NZ), lax.rem(table, NZ)
    half = NY // 2
    partner = (x * 2 + 1 - c, table)
    ahead = (lax.rem(x + 1, NX) * 2 + c, table)
    behind = (lax.rem(x + NX - 1, NX) * 2 + c, table)
    sides = (ahead, behind)

    def dz_of(s):
        odd = lax.rem(s, 2)
        return lax.rem(NZ // 2 + (1 - 2 * odd) * lax.div(s + 1, 2), NZ)

    def tile_of(s, i):
        return lax.rem(y + i, NY) * NZ + lax.rem(z + dz_of(s), NZ)

    def source_of(s, i):
        return lax.rem(y + NY - i, NY) * NZ + lax.rem(z + NZ - dz_of(s), NZ)

    barrier = pltpu.get_barrier_semaphore()

    def greet(k, carry):
        pl.semaphore_signal(
            barrier, inc=1, device_id=(dp, lax.rem(table + k, NY * NZ)), device_id_type=MESH
        )
        return carry

    for peer in (partner, ahead, behind):
        pl.semaphore_signal(barrier, inc=1, device_id=peer, device_id_type=MESH)
    lax.fori_loop(1, NY * NZ, greet, 0)

    def grad_copy(k):
        r = k % NX
        core = (1 - c) if k < NX else c
        block = lax.rem(x + r, NX) * 2 + core
        return pltpu.make_async_copy(
            gt_ref.at[pl.ds(pl.multiple_of(block * ROWS, ROWS), ROWS), :],
            grads.at[pl.ds(k * ROWS, ROWS), :],
            grad_sem.at[k],
        )

    def coef_copy(s, i):
        slot = lax.rem(s, 2)
        return pltpu.make_async_copy(
            coef_ref.at[tile_of(s, i)],
            coefs.at[slot, :, pl.ds(i * ROWS, ROWS)],
            coef_sem.at[slot, i],
        )

    def pair_copy(q):
        return pltpu.make_async_remote_copy(
            src_ref=pair_out.at[q], dst_ref=pair_in.at[q],
            send_sem=pair_send.at[q], recv_sem=pair_recv.at[q],
            device_id=partner, device_id_type=MESH,
        )

    def opp_copy(q, side):
        return pltpu.make_async_remote_copy(
            src_ref=opp_out.at[q, side], dst_ref=opp_in.at[q, side],
            send_sem=opp_send.at[q, side], recv_sem=opp_recv.at[q, side],
            device_id=sides[side], device_id_type=MESH,
        )

    def near_copy(q, side, part):
        return pltpu.make_async_remote_copy(
            src_ref=near_out.at[q, side, part], dst_ref=near_in.at[q, side, part],
            send_sem=near_send.at[q, side, part], recv_sem=near_recv.at[q, side, part],
            device_id=sides[side], device_id_type=MESH,
        )

    def tile_copy(s, i):
        return pltpu.make_async_remote_copy(
            src_ref=tiles.at[s, i], dst_ref=got.at[s, i],
            send_sem=tile_send.at[s, i], recv_sem=tile_recv.at[s, i],
            device_id=(dp, tile_of(s, i)), device_id_type=MESH,
        )

    for i in range(NY):
        coef_copy(0, i).start()
    for k in range(2 * NX):
        grad_copy(k).start()
    for k in range(2 * NX):
        grad_copy(k).wait()
    acc[...] = jnp.zeros_like(acc)

    def product(s, which):
        return jnp.dot(
            grads[which * NX * ROWS : (which + 1) * NX * ROWS, :], coefs[lax.rem(s, 2)],
            preferred_element_type=F32,
        )

    def stage1(s):
        @pl.when(s + 1 < NZ)
        def _():
            for i in range(NY):
                coef_copy(s + 1, i).start()

        for i in range(NY):
            coef_copy(s, i).wait()
        theirs = product(s, 0).astype(BF)
        for r in range(NX):
            for i in range(NY):
                pair_out[s, r, i] = theirs[r * ROWS : (r + 1) * ROWS, i * ROWS : (i + 1) * ROWS]

        @pl.when(s == 0)
        def _():
            pl.semaphore_wait(barrier, NY * NZ + 2)

        pair_copy(s).start()
        mine = product(s, 1)
        slot = lax.rem(s, 2)
        for r in range(NX):
            for i in range(NY):
                own[slot, r, i] = mine[r * ROWS : (r + 1) * ROWS, i * ROWS : (i + 1) * ROWS]

    def stage2(q):
        pair_copy(q).wait_recv()
        slot = lax.rem(q, 2)
        four = lax.rem(q, 4)

        def summed(r, lo):
            return own[slot, r, lo : lo + half] + pair_in[q, r, lo : lo + half].astype(F32)

        for side in range(2):
            opp_out[q, side] = summed(2, side * half).astype(BF)
            opp_copy(q, side).start()
        for side in range(2):
            r = 1 if side == 0 else NX - 1
            near_out[q, side, 0] = summed(r, (1 - side) * half).astype(BF)
            near_copy(q, side, 0).start()
        for side in range(2):
            r = 1 if side == 0 else NX - 1
            keep[slot, side] = summed(r, side * half)
        for part in range(2):
            fin0[four, part * half : (part + 1) * half] = summed(0, part * half)

    def stage3(q):
        slot = lax.rem(q, 2)
        for side in range(2):
            opp_copy(q, side).wait_recv()
            near_out[q, side, 1] = (keep[slot, side] + opp_in[q, side].astype(F32)).astype(BF)
            near_copy(q, side, 1).start()

    def stage4(q):
        four = lax.rem(q, 4)
        for side in range(2):
            for part in range(2):
                near_copy(q, side, part).wait_recv()
        for h in range(2):
            lo = h * half
            total = fin0[four, lo : lo + half]
            for side in range(2):
                part = 1 if side == h else 0
                total = total + near_in[q, side, part].astype(F32)
            tiles[q, lo : lo + half] = total.astype(BF)
        for i in range(NY):
            if i == 0:
                @pl.when(q < NZ - 1)
                def _():
                    tile_copy(q, 0).start()
            else:
                tile_copy(q, i).start()

    def step(s, carry):
        pl.when(s < NZ)(lambda: stage1(s))
        pl.when((s >= 1) & (s < NZ + 1))(lambda: stage2(s - 1))
        pl.when((s >= 2) & (s < NZ + 2))(lambda: stage3(s - 2))
        pl.when(s >= 3)(lambda: stage4(s - 3))
        return carry

    lax.fori_loop(0, NZ + 3, step, 0)

    def gather(s, carry):
        for i in range(NY):
            if i == 0:
                @pl.when(s < NZ - 1)
                def _():
                    tile_copy(s, 0).wait_recv()

                @pl.when(s == NZ - 1)
                def _():
                    got[s, 0] = tiles[s, 0]
            else:
                tile_copy(s, i).wait_recv()
        slots = [slots_ref[source_of(s, i), table] for i in range(NY)]
        parts = [got[s, i].astype(F32) for i in range(NY)]
        for k in range(OWN):
            total = acc[k]
            for i in range(NY):
                total = total + jnp.where(slots[i] == k, parts[i], 0.0)
            acc[k] = total
        return carry

    lax.fori_loop(0, NZ, gather, 0)
    for k in range(OWN):
        out_ref[k * ROWS : (k + 1) * ROWS, :] = acc[k].T.astype(BF)

    def drain(q, carry):
        pair_copy(q).wait_send()
        for side in range(2):
            opp_copy(q, side).wait_send()
            for part in range(2):
                near_copy(q, side, part).wait_send()
        for i in range(NY):
            if i == 0:
                @pl.when(q < NZ - 1)
                def _():
                    tile_copy(q, 0).wait_send()
            else:
                tile_copy(q, i).wait_send()
        return carry

    lax.fori_loop(0, NZ, drain, 0)


def exchange(slots, coef, grads):
    tokens = coef.shape[1]
    half = NY // 2
    tile = (ROWS, ROWS)
    dma = pltpu.SemaphoreType.DMA
    return pl.pallas_call(
        exchange_kernel,
        in_specs=[
            pl.BlockSpec(memory_space=pltpu.SMEM),
            pl.BlockSpec(memory_space=pl.ANY),
            pl.BlockSpec(memory_space=pl.ANY),
        ],
        out_specs=pl.BlockSpec(memory_space=pltpu.VMEM),
        out_shape=jax.ShapeDtypeStruct((OWN * ROWS, ROWS), BF),
        scratch_shapes=[
            pltpu.VMEM((2 * NX * ROWS, tokens), BF),
            pltpu.VMEM((2, tokens, NY * ROWS), BF),
            pltpu.VMEM((2, NX, NY) + tile, F32),
            pltpu.VMEM((NZ, NX, NY) + tile, BF),
            pltpu.VMEM((NZ, NX, NY) + tile, BF),
            pltpu.VMEM((NZ, 2, half) + tile, BF),
            pltpu.VMEM((NZ, 2, half) + tile, BF),
            pltpu.VMEM((NZ, 2, 2, half) + tile, BF),
            pltpu.VMEM((NZ, 2, 2, half) + tile, BF),
            pltpu.VMEM((2, 2, half) + tile, F32),
            pltpu.VMEM((4, NY) + tile, F32),
            pltpu.VMEM((NZ, NY) + tile, BF),
            pltpu.VMEM((NZ, NY) + tile, BF),
            pltpu.VMEM((OWN,) + tile, F32),
            dma((2 * NX,)),
            dma((2, NY)),
            dma((NZ,)),
            dma((NZ,)),
            dma((NZ, 2)),
            dma((NZ, 2)),
            dma((NZ, 2, 2)),
            dma((NZ, 2, 2)),
            dma((NZ, NY)),
            dma((NZ, NY)),
        ],
        compiler_params=pltpu.CompilerParams(
            collective_id=0, has_side_effects=True, vmem_limit_bytes=60 << 20
        ),
        name="exchange",
    )(slots, coef, grads)


def body(out_grad, pair_cells, weight_codes, head_scale, touch_slots):
    tokens = out_grad.shape[0]
    pairs = pair_cells.shape[1] * pair_cells.shape[2]
    cells = pair_cells.transpose(1, 2, 0).reshape(pairs, tokens)
    codes = weight_codes.transpose(1, 2, 0).reshape(pairs, tokens)
    coef, grads = coef_tables(cells, codes, head_scale, out_grad)
    return exchange(touch_slots.reshape(touch_slots.shape[0], -1), coef, grads)


def solution(mesh):
    return jax.shard_map(
        body,
        mesh=mesh,
        in_specs=(
            P(("dp", "table"), None),
            P(("dp", "table"), None, None),
            P(("dp", "table"), None, None),
            P(),
            P(),
        ),
        out_specs=P("table", "dp"),
        check_vma=False,
    )
```

time: 271 us -> 79.9 us (0.29)
  matrix products: 111 us -> 0 us
  waiting for transfers between devices: 85 us -> 0 us
  Pallas kernels: 0 us -> 73.5 us
  local copies, waits for them, and re-layouts: 38.7 us -> 6.12 us
  between operations: 13.4 us -> 0.01 us
  other arithmetic: 11.7 us -> 0 us
  starting transfers between devices: 10.1 us -> 0 us
    dot_general x11 -> x0, matrix products: 111 us -> none  [the longest x8 79.5 us: build(): jnp.einsum('tpj,tpr->tjr', tile_hot, row_hot, precision=lax.Precision.HIG...]
    pallas_call x0 -> x2, Pallas kernels: none -> 73.5 us  [the longest x1 56.6 us: exchange(): pl.pallas_call(exchange_kernel, in_specs=[pl.BlockSpec(memory_space=pltpu...]
    unnamed x2 -> x0, waiting for transfers between devices: 57.7 us -> none
    all_to_all x1 -> x0, waiting for transfers between devices: 27.3 us -> none  [body(): lax.all_to_all(sent.astype(jnp.bfloat16), 'table', split_axis=0, concat_a...]
    all_to_all x1 -> x0, starting transfers between devices: 10.1 us -> none  [body(): lax.all_to_all(sent.astype(jnp.bfloat16), 'table', split_axis=0, concat_a...]
    convert_element_type x1 -> x0, other arithmetic: 9.1 us -> none  [body(): partial_value.astype(jnp.bfloat16)]
    dynamic_update_slice x8 -> x0, local copies, waits for them, and re-layouts: 8.53 us -> none  [coef_table(): lax.map(build, (cell_block.reshape(block // inner, inner, pairs), weight_...]
    dynamic_slice x9 -> x0, local copies, waits for them, and re-layouts: 7.72 us -> none  [the longest x8 6.99 us: tile_partial(): lax.scan(accumulate, jnp.zeros((span, width), jnp.float32), (cell_blocks,...]
  transfers between devices with their start and end apart: 2 -> 0, of which waited for: 2 -> 0; matrix products, arithmetic and copies ran while one was open for 0% -> 0% of each run, Pallas kernels for 0% -> 0%
where the time goes in v1:
time: 79.9 us; the launch traced here: 79.6 us
  Pallas kernels  73.5 us (92%)
  local copies, waits for them, and re-layouts  6.12 us (8%)
    pallas_call x1, Pallas kernels, exchange(): pl.pallas_call(exchange_kernel, in_specs=[pl.BlockSpec(memory_space=pltpu...  56.6 us
    pallas_call x1, Pallas kernels, coef_tables(): pl.pallas_call(functools.partial(coef_kernel, block, unroll, stride), gri...  16.9 us
    unnamed x9, local copies, waits for them, and re-layouts  6.12 us

profile of v1, /device:TPU:32, one launch (start us, length us, event | category | flops | bytes accessed | tf_op | source)
XLA Modules:
  0.0 79.6 jit_solution(11861160981244470964)
XLA Ops:
  0.0 0.0 copy-start.1
  0.0 1.2 %copy-done.1 = s32[1024,8,32]{0,2,1:T(8,128)S(1)} copy-done((s32[1024,8,32]{0,2,1:T(8,128)S(1)}, s32[1024,8,32]{0,2,1:T(8,128)}, u32[]{:S(2)}) %copy-start.1) | copy-done | bytes 1048600
  1.2 0.0 copy-start.2
  1.2 1.2 %copy-done.2 = s32[1024,8,32]{0,2,1:T(8,128)S(1)} copy-done((s32[1024,8,32]{0,2,1:T(8,128)S(1)}, s32[1024,8,32]{0,2,1:T(8,128)}, u32[]{:S(2)}) %copy-start.2) | copy-done | bytes 1048600
  2.5 0.0 copy-start.3
  2.5 0.7 copy-done.3
  3.1 16.9 %coef_tables.1 = (bf16[32,1024,128]{2,1,0:T(8,128)(2,1)}, bf16[1024,1024]{1,0:T(8,128)(2,1)S(1)}) custom-call(f32[8]{0:T(128)S(1)} %copy-done.3, s32[256,1024]{1,0:T(8,128)S(1)} %bitcast.7, s32[256,1024]{1,0:T(8,128)S(1)} %bitcast.8, bf16[1024,1024]{1,0:T(8,128)(2,1)} %grad_ref.1), custom_call_target="tpu_custom_call" | custom-call | tf_op jit(solution)/shard_map/coef_tables/pallas_call | solution.py:76
  20.0 0.0 copy-start
  20.0 1.3 %copy-done = bf16[1024,1024]{1,0:T(8,128)(2,1)} copy-done((bf16[1024,1024]{1,0:T(8,128)(2,1)}, bf16[1024,1024]{1,0:T(8,128)(2,1)S(1)}, u32[]{:S(2)}) %copy-start) | copy-done | bytes 2097176
  21.3 56.6 %exchange.1 = bf16[1024,128]{1,0:T(8,128)(2,1)} custom-call(s32[32,32]{1,0:T(8,128)} %bitcast.9, bf16[32,1024,128]{2,1,0:T(8,128)(2,1)} %get-tuple-element.7.coef_ref, bf16[1024,1024]{1,0:T(8,128)(2,1)} %copy-done), custom_call_target="tpu_custom_call" | custom-call | tf_op jit(solution)/shard_map/exchange/pallas_call | solution.py:326
  78.0 1.7 %copy.7 = bf16[1024,128]{1,0:T(8,128)(2,1)} copy(bf16[1024,128]{1,0:T(8,128)(2,1)} %exchange.1) | data formatting | bytes 524288
Async XLA Ops:
  0.0 1.2 %copy-start.1 = (s32[1024,8,32]{0,2,1:T(8,128)S(1)}, s32[1024,8,32]{0,2,1:T(8,128)}, u32[]{:S(2)}) copy-start(s32[1024,8,32]{0,2,1:T(8,128)} %param.6) | copy-start | bytes 3145732
  1.2 1.2 %copy-start.2 = (s32[1024,8,32]{0,2,1:T(8,128)S(1)}, s32[1024,8,32]{0,2,1:T(8,128)}, u32[]{:S(2)}) copy-start(s32[1024,8,32]{0,2,1:T(8,128)} %param.7) | copy-start | bytes 3145732
  2.5 0.7 copy-start.3
  20.0 1.3 %copy-start = (bf16[1024,1024]{1,0:T(8,128)(2,1)}, bf16[1024,1024]{1,0:T(8,128)(2,1)S(1)}, u32[]{:S(2)}) copy-start(bf16[1024,1024]{1,0:T(8,128)(2,1)S(1)} %get-tuple-element.8.gt_ref) | copy-start | bytes 6291460

commit v2 on v0

v2 whole, which is shorter than its diff:
```python
import functools

import jax
import jax.numpy as jnp
from jax import lax
from jax.experimental import pallas as pl
from jax.experimental.pallas import tpu as pltpu
from jax.sharding import PartitionSpec as P

ROWS = 128
TOUCH = 32
OWN = 8
NX = 4
NY = 4
NZ = 8
PARTS = 2
PART = ROWS // PARTS
PAIRED = TOUCH // PARTS
BLOCK = 128
STRIDE = BLOCK + 8
STEPS = PARTS * NZ
MESH = pl.DeviceIdType.MESH
BF = jnp.bfloat16
F32 = jnp.float32


def kernel(scale_ref, slots_ref, cells_hbm, codes_hbm, grad_hbm, out_ref,
           cells, codes, grad, row_of, tile_of_pair, weight_of, table, coefs, grads,
           own, pair_out, pair_in, opp_out, opp_in, near_out, near_in, keep, fin0, tiles, got, acc,
           cell_sem, code_sem, grad_sem, pair_send, pair_recv,
           opp_send, opp_recv, near_send, near_recv, tile_send, tile_recv):
    dp = lax.axis_index("dp")
    group = lax.axis_index("table")
    x, c = lax.div(dp, 2), lax.rem(dp, 2)
    y, z = lax.div(group, NZ), lax.rem(group, NZ)
    pairs, tokens = cells.shape
    heads = scale_ref.shape[0]
    per = pairs // heads
    blocks = tokens // BLOCK
    partner = (x * 2 + 1 - c, group)
    ahead = (lax.rem(x + 1, NX) * 2 + c, group)
    behind = (lax.rem(x + NX - 1, NX) * 2 + c, group)
    sides = (ahead, behind)

    def dz_of(s):
        zz = lax.rem(s, NZ)
        odd = lax.rem(zz, 2)
        return lax.rem(NZ // 2 + (1 - 2 * odd) * lax.div(zz + 1, 2), NZ)

    def z_of(s):
        return lax.rem(z + dz_of(s), NZ)

    def source_of(s, i):
        return i * NZ + lax.rem(z + NZ - dz_of(s), NZ)

    def block_start(b):
        return pl.multiple_of(b * BLOCK, BLOCK)

    barrier = pltpu.get_barrier_semaphore()

    def greet(k, carry):
        pl.semaphore_signal(
            barrier, inc=1, device_id=(dp, lax.rem(group + k, NY * NZ)), device_id_type=MESH
        )
        return carry

    def cell_copy(b):
        cut = pl.ds(block_start(b), BLOCK)
        return pltpu.make_async_copy(cells_hbm.at[:, cut], cells.at[:, cut], cell_sem.at[b])

    def code_copy(b):
        cut = pl.ds(block_start(b), BLOCK)
        return pltpu.make_async_copy(codes_hbm.at[:, cut], codes.at[:, cut], code_sem.at[b])

    def grad_copy(b):
        cut = pl.ds(block_start(b), BLOCK)
        return pltpu.make_async_copy(grad_hbm.at[cut, :], grad.at[cut, :], grad_sem.at[b])

    for b in range(blocks):
        cell_copy(b).start()
        code_copy(b).start()
        grad_copy(b).start()
    for peer in (partner, ahead, behind):
        pl.semaphore_signal(barrier, inc=1, device_id=peer, device_id_type=MESH)
    lax.fori_loop(1, NY * NZ, greet, 0)
    acc[...] = jnp.zeros_like(acc)

    def pair_copy(q):
        return pltpu.make_async_remote_copy(
            src_ref=pair_out.at[q], dst_ref=pair_in.at[q],
            send_sem=pair_send.at[q], recv_sem=pair_recv.at[q],
            device_id=partner, device_id_type=MESH,
        )

    def opp_copy(q, side):
        return pltpu.make_async_remote_copy(
            src_ref=opp_out.at[q, side], dst_ref=opp_in.at[q, side],
            send_sem=opp_send.at[q, side], recv_sem=opp_recv.at[q, side],
            device_id=sides[side], device_id_type=MESH,
        )

    def near_copy(q, side, part):
        return pltpu.make_async_remote_copy(
            src_ref=near_out.at[q, side, part], dst_ref=near_in.at[q, side, part],
            send_sem=near_send.at[q, side, part], recv_sem=near_recv.at[q, side, part],
            device_id=sides[side], device_id_type=MESH,
        )

    def tile_copy(s, i):
        return pltpu.make_async_remote_copy(
            src_ref=tiles.at[s, i], dst_ref=got.at[s, y],
            send_sem=tile_send.at[s, i], recv_sem=tile_recv.at[s, y],
            device_id=(dp, i * NZ + z_of(s)), device_id_type=MESH,
        )

    def tile_arrival(s, i):
        return pltpu.make_async_remote_copy(
            src_ref=tiles.at[s, i], dst_ref=got.at[s, i],
            send_sem=tile_send.at[s, i], recv_sem=tile_recv.at[s, i],
            device_id=(dp, i * NZ + z_of(s)), device_id_type=MESH,
        )

    def stays(s, i):
        return (dz_of(s) == 0) & (y == i)

    def prepare(b):
        cell_copy(b).wait()
        code_copy(b).wait()
        cut = pl.ds(block_start(b), BLOCK)
        cell = cells[:, cut]
        row_of[cut, :] = (cell & (ROWS - 1)).astype(F32).astype(BF).T
        tile_of_pair[cut, :] = (cell >> 7).astype(F32).astype(BF).T
        weight = jnp.concatenate(
            [
                codes[h * per : (h + 1) * per, cut].astype(F32) * (scale_ref[h] / 128.0)
                for h in range(heads)
            ],
            axis=0,
        )
        weight_of[cut, :] = weight.astype(BF).T
        grad_copy(b).wait()
        for k in range(2 * NX):
            core = (1 - c) if k < NX else c
            block = lax.rem(x + k % NX, NX) * 2 + core
            columns = pl.ds(pl.multiple_of(block * ROWS, ROWS), ROWS)
            grads[k * ROWS : (k + 1) * ROWS, cut] = grad[cut, columns].T

    row_iota = lax.broadcasted_iota(jnp.int32, (PART, pairs), 0).astype(F32).astype(BF)
    tile_iota = lax.broadcasted_iota(jnp.int32, (TOUCH, pairs), 0).astype(F32).astype(BF)
    one = jnp.ones((), BF)
    zero = jnp.zeros((), BF)

    def coefficients(t):
        part = lax.div(t, blocks)
        start = block_start(lax.rem(t, blocks))
        shift = (part * PART).astype(F32).astype(BF)
        for v in range(BLOCK // 16):
            sixteen = pl.ds(pl.multiple_of(start + v * 16, 16), 16)
            row = row_of[sixteen, :] - shift
            tile = tile_of_pair[sixteen, :]
            weights = weight_of[sixteen, :]
            for u in range(16):
                row_hot = jnp.where(
                    jnp.broadcast_to(row[u : u + 1, :], (PART, pairs)) == row_iota, one, zero
                ).astype(jnp.float8_e4m3fn)
                tile_hot = jnp.where(
                    jnp.broadcast_to(tile[u : u + 1, :], (TOUCH, pairs)) == tile_iota,
                    jnp.broadcast_to(weights[u : u + 1, :], (TOUCH, pairs)),
                    zero,
                )
                result = lax.dot_general(
                    tile_hot, row_hot, (((1,), (1,)), ((), ())), preferred_element_type=F32
                )
                table[pl.ds(v * 16 + u, PAIRED, stride=STRIDE), :] = jnp.concatenate(
                    [result[k * PAIRED : (k + 1) * PAIRED] for k in range(PARTS)], axis=1
                )
        for j in range(PAIRED):
            coefs[part * PAIRED + j, pl.ds(start, BLOCK), :] = table[
                j * STRIDE : j * STRIDE + BLOCK, :
            ].astype(BF)

    def product(s, which):
        first = lax.div(s, NZ) * PAIRED + z_of(s)
        operand = jnp.concatenate([coefs[first], coefs[first + NZ]], axis=1)
        return jnp.dot(
            grads[which * NX * ROWS : (which + 1) * NX * ROWS, :], operand,
            preferred_element_type=F32,
        )

    def stage1(s):
        theirs = product(s, 0).astype(BF)
        for r in range(NX):
            for i in range(2):
                pair_out[s, r, i] = theirs[r * ROWS : (r + 1) * ROWS, i * ROWS : (i + 1) * ROWS]

        @pl.when(s == 0)
        def _():
            pl.semaphore_wait(barrier, NY * NZ + 2)

        pair_copy(s).start()
        mine = product(s, 1)
        slot = lax.rem(s, 2)
        for r in range(NX):
            for i in range(2):
                own[slot, r, i] = mine[r * ROWS : (r + 1) * ROWS, i * ROWS : (i + 1) * ROWS]

    def stage2(q):
        pair_copy(q).wait_recv()
        slot = lax.rem(q, 2)
        four = lax.rem(q, 4)

        def summed(r, i):
            return own[slot, r, i] + pair_in[q, r, i].astype(F32)

        for side in range(2):
            opp_out[q, side] = summed(2, side).astype(BF)
            opp_copy(q, side).start()
        for side in range(2):
            r = 1 if side == 0 else NX - 1
            near_out[q, side, 0] = summed(r, 1 - side).astype(BF)
            near_copy(q, side, 0).start()
        for side in range(2):
            r = 1 if side == 0 else NX - 1
            keep[slot, side] = summed(r, side)
        for i in range(2):
            fin0[four, i] = summed(0, i)

    def stage3(q):
        slot = lax.rem(q, 2)
        for side in range(2):
            opp_copy(q, side).wait_recv()
            near_out[q, side, 1] = (keep[slot, side] + opp_in[q, side].astype(F32)).astype(BF)
            near_copy(q, side, 1).start()

    def stage4(q):
        four = lax.rem(q, 4)
        for side in range(2):
            for part in range(2):
                near_copy(q, side, part).wait_recv()
        for i in range(2):
            total = fin0[four, i]
            for side in range(2):
                total = total + near_in[q, side, 1 if side == i else 0].astype(F32)
            total = total.T.astype(BF)
            for k in range(PARTS):
                tiles[q, i + 2 * k] = total[k * PART : (k + 1) * PART]
        for i in range(NY):
            @pl.when(jnp.logical_not(stays(q, i)))
            def _():
                tile_copy(q, i).start()

    def gather(s):
        for i in range(NY):
            @pl.when(jnp.logical_not(stays(s, i)))
            def _():
                tile_arrival(s, i).wait_recv()

            @pl.when(stays(s, i))
            def _():
                got[s, i] = tiles[s, i]

        slots = [slots_ref[source_of(s, i), group] for i in range(NY)]
        parts = [got[s, i].astype(F32) for i in range(NY)]
        half = lax.div(s, NZ)
        for k in range(OWN):
            total = acc[k, half]
            for i in range(NY):
                total = total + jnp.where(slots[i] == k, parts[i], 0.0)
            acc[k, half] = total

    lag = 6

    def step(t, carry):
        s = t - blocks
        pl.when(t < blocks)(lambda: prepare(t))
        pl.when((s >= 0) & (s < STEPS))(lambda: stage1(s))
        pl.when(t < PARTS * blocks)(lambda: coefficients(t))
        pl.when((s >= 1) & (s < STEPS + 1))(lambda: stage2(s - 1))
        pl.when((s >= 2) & (s < STEPS + 2))(lambda: stage3(s - 2))
        pl.when((s >= 3) & (s < STEPS + 3))(lambda: stage4(s - 3))
        pl.when(s >= lag)(lambda: gather(s - lag))
        return carry

    lax.fori_loop(0, blocks + STEPS + lag, step, 0)

    for k in range(OWN):
        for h in range(PARTS):
            out_ref[k * ROWS + h * PART : k * ROWS + (h + 1) * PART, :] = acc[k, h].astype(BF)

    def drain(q, carry):
        pair_copy(q).wait_send()
        for side in range(2):
            opp_copy(q, side).wait_send()
            for part in range(2):
                near_copy(q, side, part).wait_send()
        for i in range(NY):
            @pl.when(jnp.logical_not(stays(q, i)))
            def _():
                tile_arrival(q, i).wait_send()
        return carry

    lax.fori_loop(0, STEPS, drain, 0)


def body(out_grad, pair_cells, weight_codes, head_scale, touch_slots):
    tokens, width = out_grad.shape
    pairs = pair_cells.shape[1] * pair_cells.shape[2]
    cells = pair_cells.transpose(1, 2, 0).reshape(pairs, tokens)
    codes = weight_codes.transpose(1, 2, 0).reshape(pairs, tokens)
    blocks = tokens // BLOCK
    square = (ROWS, ROWS)
    piece = (PART, ROWS)
    dma = pltpu.SemaphoreType.DMA
    smem = pl.BlockSpec(memory_space=pltpu.SMEM)
    hbm = pl.BlockSpec(memory_space=pltpu.HBM)
    return pl.pallas_call(
        kernel,
        in_specs=[smem, smem, hbm, hbm, hbm],
        out_specs=pl.BlockSpec(memory_space=pltpu.VMEM),
        out_shape=jax.ShapeDtypeStruct((OWN * ROWS, ROWS), BF),
        scratch_shapes=[
            pltpu.VMEM((pairs, tokens), jnp.int32),
            pltpu.VMEM((pairs, tokens), jnp.int32),
            pltpu.VMEM((tokens, width), BF),
            pltpu.VMEM((tokens, pairs), BF),
            pltpu.VMEM((tokens, pairs), BF),
            pltpu.VMEM((tokens, pairs), BF),
            pltpu.VMEM((PAIRED * STRIDE, ROWS), F32),
            pltpu.VMEM((PARTS * PAIRED, tokens, ROWS), BF),
            pltpu.VMEM((width, tokens), BF),
            pltpu.VMEM((2, NX, 2) + square, F32),
            pltpu.VMEM((STEPS, NX, 2) + square, BF),
            pltpu.VMEM((STEPS, NX, 2) + square, BF),
            pltpu.VMEM((STEPS, 2) + square, BF),
            pltpu.VMEM((STEPS, 2) + square, BF),
            pltpu.VMEM((STEPS, 2, 2) + square, BF),
            pltpu.VMEM((STEPS, 2, 2) + square, BF),
            pltpu.VMEM((2, 2) + square, F32),
            pltpu.VMEM((4, 2) + square, F32),
            pltpu.VMEM((STEPS, NY) + piece, BF),
            pltpu.VMEM((STEPS, NY) + piece, BF),
            pltpu.VMEM((OWN, PARTS) + piece, F32),
            dma((blocks,)),
            dma((blocks,)),
            dma((blocks,)),
            dma((STEPS,)),
            dma((STEPS,)),
            dma((STEPS, 2)),
            dma((STEPS, 2)),
            dma((STEPS, 2, 2)),
            dma((STEPS, 2, 2)),
            dma((STEPS, NY)),
            dma((STEPS, NY)),
        ],
        compiler_params=pltpu.CompilerParams(
            collective_id=0, has_side_effects=True, vmem_limit_bytes=60 << 20
        ),
        name="value_grad",
    )(head_scale, touch_slots.reshape(touch_slots.shape[0], -1), cells, codes, out_grad)


def solution(mesh):
    return jax.shard_map(
        body,
        mesh=mesh,
        in_specs=(
            P(("dp", "table"), None),
            P(("dp", "table"), None, None),
            P(("dp", "table"), None, None),
            P(),
            P(),
        ),
        out_specs=P("table", "dp"),
        check_vma=False,
    )
```

time: 271 us -> 86.5 us (0.32)
  matrix products: 111 us -> 0 us
  waiting for transfers between devices: 85 us -> 0 us
  Pallas kernels: 0 us -> 83.3 us
  local copies, waits for them, and re-layouts: 38.7 us -> 1.67 us
  between operations: 13.4 us -> 0.01 us
  other arithmetic: 11.7 us -> 0 us
  starting transfers between devices: 10.1 us -> 0 us
    dot_general x11 -> x0, matrix products: 111 us -> none  [the longest x8 79.5 us: build(): jnp.einsum('tpj,tpr->tjr', tile_hot, row_hot, precision=lax.Precision.HIG...]
    pallas_call x0 -> x1, Pallas kernels: none -> 83.3 us  [body(): pl.pallas_call(kernel, in_specs=[smem, smem, hbm, hbm, hbm], out_specs=pl...]
    unnamed x2 -> x0, waiting for transfers between devices: 57.7 us -> none
    all_to_all x1 -> x0, waiting for transfers between devices: 27.3 us -> none  [body(): lax.all_to_all(sent.astype(jnp.bfloat16), 'table', split_axis=0, concat_a...]
    unnamed x4 -> x1, local copies, waits for them, and re-layouts: 13.6 us -> 1.67 us
    all_to_all x1 -> x0, starting transfers between devices: 10.1 us -> none  [body(): lax.all_to_all(sent.astype(jnp.bfloat16), 'table', split_axis=0, concat_a...]
    convert_element_type x1 -> x0, other arithmetic: 9.1 us -> none  [body(): partial_value.astype(jnp.bfloat16)]
    dynamic_update_slice x8 -> x0, local copies, waits for them, and re-layouts: 8.53 us -> none  [coef_table(): lax.map(build, (cell_block.reshape(block // inner, inner, pairs), weight_...]
  transfers between devices with their start and end apart: 2 -> 0, of which waited for: 2 -> 0; matrix products, arithmetic and copies ran while one was open for 0% -> 0% of each run, Pallas kernels for 0% -> 0%
where the time goes in v2:
time: 86.5 us; the launch traced here: 85 us
  Pallas kernels  83.3 us (96%)
  local copies, waits for them, and re-layouts  1.67 us (2%)
    pallas_call x1, Pallas kernels, body(): pl.pallas_call(kernel, in_specs=[smem, smem, hbm, hbm, hbm], out_specs=pl...  83.3 us

profile of v2, /device:TPU:32, one launch (start us, length us, event | category | flops | bytes accessed | tf_op | source)
XLA Modules:
  0.0 85.0 jit_solution(15407283131186326432)
XLA Ops:
  0.0 83.3 %value_grad.1 = bf16[1024,128]{1,0:T(8,128)(2,1)} custom-call(f32[8]{0:T(128)} %scale_ref.1, s32[32,32]{1,0:T(8,128)} %bitcast.9, s32[256,1024]{1,0:T(8,128)} %bitcast.7, s32[256,1024]{1,0:T(8,128)} %bitcast.8, bf16[1024,1024]{1,0:T(8,128)(2,1)} %grad_hbm.1), custom_call_target="tpu_custom_call" | custom-call | tf_op jit(solution)/shard_map/value_grad/pallas_call | solution.py:316
  83.4 1.7 %copy.7 = bf16[1024,128]{1,0:T(8,128)(2,1)} copy(bf16[1024,128]{1,0:T(8,128)(2,1)} %value_grad.1) | data formatting | bytes 524288

commit v3 on v2

--- a/solution.py
+++ b/solution.py
@@ -18,7 +18,12 @@
 PAIRED = TOUCH // PARTS
 BLOCK = 128
 STRIDE = BLOCK + 8
-STEPS = PARTS * NZ
+STEPS = PARTS * NZ // 2
+SPAN = 4
+HALF = SPAN // 2
+LAG3 = 2
+LAG4 = 3
+LAG5 = 8
 MESH = pl.DeviceIdType.MESH
 BF = jnp.bfloat16
 F32 = jnp.float32
@@ -42,16 +47,15 @@
     behind = (lax.rem(x + NX - 1, NX) * 2 + c, group)
     sides = (ahead, behind)
 
-    def dz_of(s):
-        zz = lax.rem(s, NZ)
-        odd = lax.rem(zz, 2)
-        return lax.rem(NZ // 2 + (1 - 2 * odd) * lax.div(zz + 1, 2), NZ)
-
-    def z_of(s):
-        return lax.rem(z + dz_of(s), NZ)
-
-    def source_of(s, i):
-        return i * NZ + lax.rem(z + NZ - dz_of(s), NZ)
+    def dz_of(s, i):
+        far = lax.rem(s, NZ // 2)
+        return lax.rem(NZ // 2 + far if i == 0 else NZ // 2 - 1 - far, NZ)
+
+    def z_of(s, i):
+        return lax.rem(z + dz_of(s, i), NZ)
+
+    def source_of(s, i, k):
+        return k * NZ + lax.rem(z + NZ - dz_of(s, i), NZ)
 
     def block_start(b):
         return pl.multiple_of(b * BLOCK, BLOCK)
@@ -106,22 +110,22 @@
             device_id=sides[side], device_id_type=MESH,
         )
 
-    def tile_copy(s, i):
-        return pltpu.make_async_remote_copy(
-            src_ref=tiles.at[s, i], dst_ref=got.at[s, y],
-            send_sem=tile_send.at[s, i], recv_sem=tile_recv.at[s, y],
-            device_id=(dp, i * NZ + z_of(s)), device_id_type=MESH,
-        )
-
-    def tile_arrival(s, i):
-        return pltpu.make_async_remote_copy(
-            src_ref=tiles.at[s, i], dst_ref=got.at[s, i],
-            send_sem=tile_send.at[s, i], recv_sem=tile_recv.at[s, i],
-            device_id=(dp, i * NZ + z_of(s)), device_id_type=MESH,
-        )
-
-    def stays(s, i):
-        return (dz_of(s) == 0) & (y == i)
+    def tile_copy(s, i, k):
+        return pltpu.make_async_remote_copy(
+            src_ref=tiles.at[s, i, k], dst_ref=got.at[s, i, y],
+            send_sem=tile_send.at[s, i, k], recv_sem=tile_recv.at[s, i, y],
+            device_id=(dp, k * NZ + z_of(s, i)), device_id_type=MESH,
+        )
+
+    def tile_arrival(s, i, k):
+        return pltpu.make_async_remote_copy(
+            src_ref=tiles.at[s, i, k], dst_ref=got.at[s, i, k],
+            send_sem=tile_send.at[s, i, k], recv_sem=tile_recv.at[s, i, k],
+            device_id=(dp, k * NZ + z_of(s, i)), device_id_type=MESH,
+        )
+
+    def stays(s, i, k):
+        return (dz_of(s, i) == 0) & (y == k)
 
     def prepare(b):
         cell_copy(b).wait()
@@ -180,8 +184,10 @@
             ].astype(BF)
 
     def product(s, which):
-        first = lax.div(s, NZ) * PAIRED + z_of(s)
-        operand = jnp.concatenate([coefs[first], coefs[first + NZ]], axis=1)
+        part = lax.div(s, NZ // 2) * PAIRED
+        operand = jnp.concatenate(
+            [coefs[part + a * NZ + z_of(s, i)] for i in range(2) for a in range(2)], axis=1
+        )
         return jnp.dot(
             grads[which * NX * ROWS : (which + 1) * NX * ROWS, :], operand,
             preferred_element_type=F32,
@@ -190,7 +196,7 @@
     def stage1(s):
         theirs = product(s, 0).astype(BF)
         for r in range(NX):
-            for i in range(2):
+            for i in range(SPAN):
                 pair_out[s, r, i] = theirs[r * ROWS : (r + 1) * ROWS, i * ROWS : (i + 1) * ROWS]
 
         @pl.when(s == 0)
@@ -201,16 +207,16 @@
         mine = product(s, 1)
         slot = lax.rem(s, 2)
         for r in range(NX):
-            for i in range(2):
+            for i in range(SPAN):
                 own[slot, r, i] = mine[r * ROWS : (r + 1) * ROWS, i * ROWS : (i + 1) * ROWS]
 
     def stage2(q):
         pair_copy(q).wait_recv()
         slot = lax.rem(q, 2)
-        four = lax.rem(q, 4)
-
-        def summed(r, i):
-            return own[slot, r, i] + pair_in[q, r, i].astype(F32)
+
+        def summed(r, half):
+            lo = half * HALF
+            return own[slot, r, lo : lo + HALF] + pair_in[q, r, lo : lo + HALF].astype(F32)
 
         for side in range(2):
             opp_out[q, side] = summed(2, side).astype(BF)
@@ -221,67 +227,76 @@
             near_copy(q, side, 0).start()
         for side in range(2):
             r = 1 if side == 0 else NX - 1
-            keep[slot, side] = summed(r, side)
-        for i in range(2):
-            fin0[four, i] = summed(0, i)
+            keep[lax.rem(q, 4), side] = summed(r, side)
+        for half in range(2):
+            fin0[lax.rem(q, 8), half] = summed(0, half)
 
     def stage3(q):
-        slot = lax.rem(q, 2)
+        slot = lax.rem(q, 4)
         for side in range(2):
             opp_copy(q, side).wait_recv()
             near_out[q, side, 1] = (keep[slot, side] + opp_in[q, side].astype(F32)).astype(BF)
             near_copy(q, side, 1).start()
 
     def stage4(q):
-        four = lax.rem(q, 4)
+        eight = lax.rem(q, 8)
         for side in range(2):
             for part in range(2):
                 near_copy(q, side, part).wait_recv()
         for i in range(2):
-            total = fin0[four, i]
+            total = fin0[eight, i]
             for side in range(2):
                 total = total + near_in[q, side, 1 if side == i else 0].astype(F32)
-            total = total.T.astype(BF)
-            for k in range(PARTS):
-                tiles[q, i + 2 * k] = total[k * PART : (k + 1) * PART]
-        for i in range(NY):
-            @pl.when(jnp.logical_not(stays(q, i)))
-            def _():
-                tile_copy(q, i).start()
+            for a in range(HALF):
+                turned = total[a].T.astype(BF)
+                for k in range(PARTS):
+                    tiles[q, i, a + HALF * k] = turned[k * PART : (k + 1) * PART]
+            for k in range(NY):
+                @pl.when(jnp.logical_not(stays(q, i, k)))
+                def _():
+                    tile_copy(q, i, k).start()
 
     def gather(s):
-        for i in range(NY):
-            @pl.when(jnp.logical_not(stays(s, i)))
-            def _():
-                tile_arrival(s, i).wait_recv()
-
-            @pl.when(stays(s, i))
-            def _():
-                got[s, i] = tiles[s, i]
-
-        slots = [slots_ref[source_of(s, i), group] for i in range(NY)]
-        parts = [got[s, i].astype(F32) for i in range(NY)]
-        half = lax.div(s, NZ)
-        for k in range(OWN):
-            total = acc[k, half]
-            for i in range(NY):
-                total = total + jnp.where(slots[i] == k, parts[i], 0.0)
-            acc[k, half] = total
-
-    lag = 6
+        for i in range(2):
+            for k in range(NY):
+                @pl.when(jnp.logical_not(stays(s, i, k)))
+                def _():
+                    tile_arrival(s, i, k).wait_recv()
+
+                @pl.when(stays(s, i, k))
+                def _():
+                    got[s, i, k] = tiles[s, i, k]
+
+        pieces = [(i, k) for i in range(2) for k in range(NY)]
+        slots = [slots_ref[source_of(s, i, k), group] for i, k in pieces]
+        parts = [got[s, i, k].astype(F32) for i, k in pieces]
+        part = lax.div(s, NZ // 2)
+        for o in range(OWN):
+            total = acc[o, part]
+            for slot, value in zip(slots, parts):
+                total = total + jnp.where(slot == o, value, 0.0)
+            acc[o, part] = total
+
+    def more(s):
+        def one_block(half, carry):
+            coefficients(blocks + half)
+            return carry
+
+        lax.fori_loop(3 * (s - 1), lax.min(3 * s, blocks), one_block, 0)
 
     def step(t, carry):
         s = t - blocks
         pl.when(t < blocks)(lambda: prepare(t))
         pl.when((s >= 0) & (s < STEPS))(lambda: stage1(s))
-        pl.when(t < PARTS * blocks)(lambda: coefficients(t))
+        pl.when(t < blocks)(lambda: coefficients(t))
         pl.when((s >= 1) & (s < STEPS + 1))(lambda: stage2(s - 1))
-        pl.when((s >= 2) & (s < STEPS + 2))(lambda: stage3(s - 2))
-        pl.when((s >= 3) & (s < STEPS + 3))(lambda: stage4(s - 3))
-        pl.when(s >= lag)(lambda: gather(s - lag))
+        pl.when((s >= LAG3) & (s < STEPS + LAG3))(lambda: stage3(s - LAG3))
+        pl.when((s >= LAG4) & (s < STEPS + LAG4))(lambda: stage4(s - LAG4))
+        pl.when(s >= LAG5)(lambda: gather(s - LAG5))
+        pl.when((s >= 1) & (s < 4))(lambda: more(s))
         return carry
 
-    lax.fori_loop(0, blocks + STEPS + lag, step, 0)
+    lax.fori_loop(0, blocks + STEPS + LAG5, step, 0)
 
     for k in range(OWN):
         for h in range(PARTS):
@@ -293,10 +308,11 @@
             opp_copy(q, side).wait_send()
             for part in range(2):
                 near_copy(q, side, part).wait_send()
-        for i in range(NY):
-            @pl.when(jnp.logical_not(stays(q, i)))
-            def _():
-                tile_arrival(q, i).wait_send()
+        for i in range(2):
+            for k in range(NY):
+                @pl.when(jnp.logical_not(stays(q, i, k)))
+                def _():
+                    tile_arrival(q, i, k).wait_send()
         return carry
 
     lax.fori_loop(0, STEPS, drain, 0)
@@ -328,17 +344,17 @@
             pltpu.VMEM((PAIRED * STRIDE, ROWS), F32),
             pltpu.VMEM((PARTS * PAIRED, tokens, ROWS), BF),
             pltpu.VMEM((width, tokens), BF),
-            pltpu.VMEM((2, NX, 2) + square, F32),
-            pltpu.VMEM((STEPS, NX, 2) + square, BF),
-            pltpu.VMEM((STEPS, NX, 2) + square, BF),
-            pltpu.VMEM((STEPS, 2) + square, BF),
-            pltpu.VMEM((STEPS, 2) + square, BF),
-            pltpu.VMEM((STEPS, 2, 2) + square, BF),
-            pltpu.VMEM((STEPS, 2, 2) + square, BF),
-            pltpu.VMEM((2, 2) + square, F32),
-            pltpu.VMEM((4, 2) + square, F32),
-            pltpu.VMEM((STEPS, NY) + piece, BF),
-            pltpu.VMEM((STEPS, NY) + piece, BF),
+            pltpu.VMEM((2, NX, SPAN) + square, F32),
+            pltpu.VMEM((STEPS, NX, SPAN) + square, BF),
+            pltpu.VMEM((STEPS, NX, SPAN) + square, BF),
+            pltpu.VMEM((STEPS, 2, HALF) + square, BF),
+            pltpu.VMEM((STEPS, 2, HALF) + square, BF),
+            pltpu.VMEM((STEPS, 2, 2, HALF) + square, BF),
+            pltpu.VMEM((STEPS, 2, 2, HALF) + square, BF),
+            pltpu.VMEM((4, 2, HALF) + square, F32),
+            pltpu.VMEM((8, 2, HALF) + square, F32),
+            pltpu.VMEM((STEPS, 2, NY) + piece, BF),
+            pltpu.VMEM((STEPS, 2, NY) + piece, BF),
             pltpu.VMEM((OWN, PARTS) + piece, F32),
             dma((blocks,)),
             dma((blocks,)),
@@ -349,8 +365,8 @@
             dma((STEPS, 2)),
             dma((STEPS, 2, 2)),
             dma((STEPS, 2, 2)),
-            dma((STEPS, NY)),
-            dma((STEPS, NY)),
+            dma((STEPS, 2, NY)),
+            dma((STEPS, 2, NY)),
         ],
         compiler_params=pltpu.CompilerParams(
             collective_id=0, has_side_effects=True, vmem_limit_bytes=60 << 20

time: 86.5 us -> 69.7 us (0.81); the launches traced: 85 us -> 69.1 us
  Pallas kernels: 83.3 us -> 67.4 us
    pallas_call x1, Pallas kernels: 83.3 us -> 67.4 us  [body(): pl.pallas_call(kernel, in_specs=[smem, smem, hbm, hbm, hbm], out_specs=pl...]
where the time goes in v3:
time: 69.7 us; the launch traced here: 69.1 us
  Pallas kernels  67.4 us (97%)
  local copies, waits for them, and re-layouts  1.67 us (2%)
    pallas_call x1, Pallas kernels, body(): pl.pallas_call(kernel, in_specs=[smem, smem, hbm, hbm, hbm], out_specs=pl...  67.4 us
    unnamed x1, local copies, waits for them, and re-layouts  1.67 us

profile of v3, /device:TPU:32, one launch (start us, length us, event | category | flops | bytes accessed | tf_op | source)
XLA Modules:
  0.0 69.1 jit_solution(838303965990787253)
XLA Ops:
  0.0 67.4 %value_grad.1 = bf16[1024,128]{1,0:T(8,128)(2,1)} custom-call(f32[8]{0:T(128)} %scale_ref.1, s32[32,32]{1,0:T(8,128)} %bitcast.9, s32[256,1024]{1,0:T(8,128)} %bitcast.7, s32[256,1024]{1,0:T(8,128)} %bitcast.8, bf16[1024,1024]{1,0:T(8,128)(2,1)} %grad_hbm.1), custom_call_target="tpu_custom_call" | custom-call | tf_op jit(solution)/shard_map/value_grad/pallas_call | solution.py:332
  67.4 1.7 %copy.7 = bf16[1024,128]{1,0:T(8,128)(2,1)} copy(bf16[1024,128]{1,0:T(8,128)(2,1)} %value_grad.1) | data formatting | bytes 524288

commit v4 on v3

--- a/solution.py
+++ b/solution.py
@@ -329,6 +329,16 @@
     dma = pltpu.SemaphoreType.DMA
     smem = pl.BlockSpec(memory_space=pltpu.SMEM)
     hbm = pl.BlockSpec(memory_space=pltpu.HBM)
+    operands = [
+        pltpu.with_memory_space_constraint(array, pltpu.HBM)
+        for array in (
+            head_scale,
+            touch_slots.reshape(touch_slots.shape[0], -1),
+            cells,
+            codes,
+            out_grad,
+        )
+    ]
     return pl.pallas_call(
         kernel,
         in_specs=[smem, smem, hbm, hbm, hbm],
@@ -369,10 +379,10 @@
             dma((STEPS, 2, NY)),
         ],
         compiler_params=pltpu.CompilerParams(
-            collective_id=0, has_side_effects=True, vmem_limit_bytes=60 << 20
+            collective_id=0, has_side_effects=True, vmem_limit_bytes=45 << 20
         ),
         name="value_grad",
-    )(head_scale, touch_slots.reshape(touch_slots.shape[0], -1), cells, codes, out_grad)
+    )(*operands)
 
 
 def solution(mesh):

time: 69.7 us -> 68 us (0.976)
  local copies, waits for them, and re-layouts: 1.67 us -> 0.71 us
  Pallas kernels: 67.4 us -> 66.7 us
    unnamed x1, local copies, waits for them, and re-layouts: 1.67 us -> 0.71 us
    pallas_call x1, Pallas kernels: 67.4 us -> 66.7 us  [body(): pl.pallas_call(kernel, in_specs=[smem, smem, hbm, hbm, hbm], out_specs=pl...]
where the time goes in v4:
time: 68 us; the launch traced here: 67.4 us
  Pallas kernels  66.7 us (98%)
  local copies, waits for them, and re-layouts  0.71 us (1%)
    pallas_call x1, Pallas kernels, body(): pl.pallas_call(kernel, in_specs=[smem, smem, hbm, hbm, hbm], out_specs=pl...  66.7 us

profile of v4, /device:TPU:32, one launch (start us, length us, event | category | flops | bytes accessed | tf_op | source)
XLA Modules:
  0.0 67.4 jit_solution(10862033226773803745)
XLA Ops:
  0.0 66.7 %value_grad.1 = bf16[1024,128]{1,0:T(8,128)(2,1)S(1)} custom-call(f32[8]{0:T(128)} %scale_ref.1, s32[32,32]{1,0:T(8,128)} %bitcast.9, s32[256,1024]{1,0:T(8,128)} %bitcast.7, s32[256,1024]{1,0:T(8,128)} %bitcast.8, bf16[1024,1024]{1,0:T(8,128)(2,1)} %grad_hbm.1), custom_call_target="tpu_custom_call" | custom-call | tf_op jit(solution)/shard_map/value_grad/pallas_call | solution.py:342
  66.7 0.7 %copy.7 = bf16[1024,128]{1,0:T(8,128)(2,1)} copy(bf16[1024,128]{1,0:T(8,128)(2,1)S(1)} %value_grad.1) | data formatting | bytes 524288
